TPU v7x, 8 devices: a whole 2x2x1 slice. The times are simulated.
8 devices in a mesh: batch: 2 (over z, y), seq: 4 (over x, core).
Axes of the slice: x: 2, y: 2, z: 1, core: 2. Of those that a mesh axis runs over, the one named last changes fastest.
Arguments:
- msa_act: bfloat16 [64, 384, 256], P(('batch', 'seq')), parts along dimension 0
- msa_mask: int32 [64, 384], P(('batch', 'seq')), parts along dimension 0
- pair_act: bfloat16 [768, 384, 128], P(('batch', 'seq')), parts along dimension 0
- w_pair_bias: bfloat16 [128, 8], replicated
- w_row_in: bfloat16 [256, 1024], replicated
- w_row_out: bfloat16 [256, 256], replicated
- w_col_in: bfloat16 [256, 576], replicated
- w_col_out: bfloat16 [256, 256], replicated
- w_trans_in: bfloat16 [256, 1024], replicated
- w_trans_out: bfloat16 [1024, 256], replicated
Outputs:
- output: bfloat16 [64, 384, 256], P('batch', 'seq'), parts along dimension 0
There are 2 independent parts. A program takes and returns all parts, laid end to end along the dimension named above; an argument that names none is the same for every part.
All inputs are finite; a program needn't handle non-finite values.
Results may differ from a plain program's by a relative error of at most 0.0153404.
Values are sent between devices in bfloat16 or wider.
A program may use at most 1 GiB of HBM per device.

v0:
```python
import jax
import jax.numpy as jnp
from jax import lax
from jax.sharding import PartitionSpec as P

LN_EPS = 1.0e-5
MASK_BIG = 1.0e9
MEAN_EPS = 1.0e-10


def layer_norm(x_in):
    x_f32 = x_in.astype(jnp.float32)
    mean_val = jnp.mean(x_f32, axis=-1, keepdims=True)
    centered = x_f32 - mean_val
    var_val = jnp.mean(centered * centered, axis=-1, keepdims=True)
    return (centered * lax.rsqrt(var_val + LN_EPS)).astype(jnp.bfloat16)


def pick_tile(n_rows, per_row):
    budget = 2 ** 22
    best_tile = 1
    for candidate in range(1, n_rows + 1):
        if n_rows % candidate == 0 and candidate * per_row <= budget:
            best_tile = candidate
    return best_tile


def row_attention(value_a7, mask_bias, bias_hij, w_row_in, w_row_out):
    n_seq, n_res, n_chans = value_a7.shape
    n_heads = bias_hij.shape[0]
    head_dim = w_row_out.shape[0] // n_heads
    qk_scale = head_dim ** -0.5
    w_row_split = w_row_in.reshape(n_chans, 4, n_heads, head_dim)
    row_proj = jnp.einsum('snc,cfhd->fsnhd', layer_norm(value_a7), w_row_split, preferred_element_type=jnp.float32).astype(jnp.bfloat16)
    tile_rows = pick_tile(n_seq, n_heads * n_res * n_res)
    n_tiles = n_seq // tile_rows
    tiled_proj = row_proj.reshape(4, n_tiles, tile_rows, n_res, n_heads, head_dim)

    def tile_body(packed):
        q_tile, k_tile, v_tile, m_tile = packed
        logits = jnp.einsum('sihd,sjhd->shij', q_tile, k_tile, preferred_element_type=jnp.float32) * qk_scale
        logits = logits + bias_hij[None] + m_tile[:, None, None, :]
        attn_probs = jax.nn.softmax(logits, axis=-1).astype(jnp.bfloat16)
        return jnp.einsum('shij,sjhd->sihd', attn_probs, v_tile, preferred_element_type=jnp.float32)

    attended = lax.map(tile_body, (tiled_proj[0], tiled_proj[1], tiled_proj[2], mask_bias.reshape(n_tiles, tile_rows, n_res)))
    attended = attended.reshape(n_seq, n_res, n_heads, head_dim)
    gated_row = (jax.nn.sigmoid(row_proj[3].astype(jnp.float32)) * attended).astype(jnp.bfloat16)
    row_update = jnp.einsum('snhd,hdc->snc', gated_row, w_row_out.reshape(n_heads, head_dim, n_chans), preferred_element_type=jnp.float32)
    return (value_a7.astype(jnp.float32) + row_update).astype(jnp.bfloat16)


def column_attention(value_a7, value_a8, w_col_in, w_col_out, n_heads):
    n_seq, n_res, n_chans = value_a7.shape
    head_ch = w_col_out.shape[0]
    head_dim = head_ch // n_heads
    col_proj = jnp.einsum('snc,cf->snf', layer_norm(value_a7), w_col_in, preferred_element_type=jnp.float32).astype(jnp.bfloat16)
    queries = col_proj[:, :, :head_ch].reshape(n_seq, n_res, n_heads, head_dim)
    col_keys = col_proj[:, :, head_ch:head_ch + head_dim]
    col_vals = col_proj[:, :, head_ch + head_dim:head_ch + 2 * head_dim]
    col_gates = col_proj[:, :, head_ch + 2 * head_dim:].reshape(n_seq, n_res, n_heads, head_dim)
    mask_f32 = value_a8.astype(jnp.float32)
    q_sum = jnp.einsum('sn,snhd->nhd', value_a8.astype(jnp.bfloat16), queries, preferred_element_type=jnp.float32)
    mask_count = jnp.sum(mask_f32, axis=0)
    q_sum, mask_count = lax.psum((q_sum, mask_count), 'seq')
    q_mean = (q_sum / (mask_count + MEAN_EPS)[:, None, None]).astype(jnp.bfloat16)
    col_logits = jnp.einsum('nhd,snd->snh', q_mean, col_keys, preferred_element_type=jnp.float32) * head_dim ** -0.5
    col_logits = col_logits + (MASK_BIG * (mask_f32 - 1.0))[:, :, None]
    loc_max = jnp.max(col_logits, axis=0)
    weights = jnp.exp(col_logits - loc_max[None])
    loc_den = jnp.sum(weights, axis=0)
    loc_num = jnp.einsum('snh,snd->nhd', weights, col_vals, preferred_element_type=jnp.float32)
    glob_max = lax.pmax(loc_max, 'seq')
    rescale = jnp.exp(loc_max - glob_max)
    glob_den, glob_num = lax.psum((loc_den * rescale, loc_num * rescale[:, :, None]), 'seq')
    col_out = glob_num / glob_den[:, :, None]
    gated_col = (jax.nn.sigmoid(col_gates.astype(jnp.float32)) * col_out[None]).astype(jnp.bfloat16)
    col_update = jnp.einsum('snhd,hdc->snc', gated_col, w_col_out.reshape(n_heads, head_dim, n_chans), preferred_element_type=jnp.float32)
    return (value_a7.astype(jnp.float32) + col_update).astype(jnp.bfloat16)


def transition(value_a7, w_trans_in, w_trans_out):
    hidden = jnp.einsum('snc,cf->snf', layer_norm(value_a7), w_trans_in, preferred_element_type=jnp.float32)
    hidden = jnp.maximum(hidden, 0.0).astype(jnp.bfloat16)
    trans_update = jnp.einsum('snf,fc->snc', hidden, w_trans_out, preferred_element_type=jnp.float32)
    return (value_a7.astype(jnp.float32) + trans_update).astype(jnp.bfloat16)


def solution(mesh):
    def local_block(value_a7, value_a8, pair_act, w_pair_bias, w_row_in, w_row_out, w_col_in, w_col_out, w_trans_in, w_trans_out):
        n_heads = w_pair_bias.shape[1]
        bias_rows = jnp.einsum('ijc,ch->hij', layer_norm(pair_act), w_pair_bias, preferred_element_type=jnp.float32).astype(jnp.bfloat16)
        bias_full = lax.all_gather(bias_rows, 'seq', axis=1, tiled=True)
        mask_bias = MASK_BIG * (value_a8.astype(jnp.float32) - 1.0)
        after_row = row_attention(value_a7, mask_bias, bias_full, w_row_in, w_row_out)
        after_col = column_attention(after_row, value_a8, w_col_in, w_col_out, n_heads)
        after_trans = transition(after_col, w_trans_in, w_trans_out)
        return lax.all_to_all(after_trans, 'seq', 1, 0, tiled=True)

    rows_spec = P(('batch', 'seq'))
    return jax.shard_map(local_block, mesh=mesh, in_specs=(rows_spec, rows_spec, rows_spec, P(), P(), P(), P(), P(), P(), P()), out_specs=P('batch', 'seq'), check_vma=False)
```

profile of v0, /device:TPU:0, one launch (start us, length us, event | category | flops | bytes accessed | tf_op | source)
XLA Modules:
  0.0 298.8 jit_solution(1719789123298502280)
XLA Ops:
  6.5 6.3 %convert_reduce_fusion = f32[96,384]{1,0:T(8,128)S(1)} fusion(bf16[96,384,128]{2,1,0:T(8,128)(2,1)} %param.14), kind=kLoop, calls=%fused_computation.29 | loop fusion | flops 9400320 | bytes 9584640 | tf_op jit(solution)/shard_map/reduce_sum | solution.py:13
  12.8 0.0 copy-start.3
  12.9 0.0 copy-start.14
  12.9 12.2 %fusion.39 = f32[96,384]{1,0:T(8,128)S(1)} fusion(bf16[96,384,128]{2,1,0:T(8,128)(2,1)} %param.14, f32[96,384]{1,0:T(8,128)S(1)} %broadcast_multiply_fusion), kind=kLoop, calls=%fused_computation.32 | loop fusion | flops 18837504 | bytes 9732096 | tf_op jit(solution)/shard_map/reduce_sum | solution.py:15
  25.2 0.0 copy-start.12
  25.2 16.5 %fusion.83 = bf16[8,96,384]{2,0,1:T(8,128)(2,1)} fusion(bf16[96,384,128]{2,1,0:T(8,128)(2,1)S(1)} %copy-done.3, f32[96,384]{1,0:T(8,128)S(1)} %add_rsqrt_fusion, f32[96,384]{1,0:T(8,128)S(1)} %broadcast_multiply_fusion, bf16[128,8]{0,1:T(8,128)(2,1)S(1)} %copy-done.14), kind=kOutput, calls=%fused_computation.86 | convolution fusion | flops 94666752 | bytes 10323968 | tf_op jit(solution)/shard_map/ijc,ch->hij/dot_general | solution.py:92
  41.7 0.0 all-gather.2.cloned.1.call-update
  41.7 0.0 all-reduce.3.cloned.1.call-start
  41.8 0.1 copy.57
  42.0 1.9 copy.51
  43.9 0.2 copy.52
  44.1 9.1 %psum.29 = f32[384]{0:T(512)S(1)} all-reduce(f32[384]{0:T(512)S(1)} %get-tuple-element.94), channel_id=1, replica_groups=mesh['batch'=2,'seq'=4] {'seq'}, use_global_device_ids=true, to_apply=%region_12.13 | all-reduce | flops 384 | bytes 3072 | tf_op jit(solution)/shard_map/psum | solution.py:65
  53.1 0.2 convert_reduce_fusion.3
  53.4 0.4 fusion.59
  53.8 1.8 convert_bitcast_fusion
  55.7 2.7 copy-done.4
  58.4 2.4 fusion.104
  60.8 4.9 %all-gather.2.cloned.1.call-done = bf16[8,384,384]{2,0,1:T(8,128)(2,1)} async-done(((bf16[8,96,384]{2,0,1:T(8,128)(2,1)}), bf16[8,384,384]{2,0,1:T(8,128)(2,1)}) %all-gather.2.cloned.1.call-update) | async-done | bytes 2359312 | tf_op jit(solution)/shard_map/all_gather | solution.py:93
  65.7 3.2 %copy.54 = bf16[8,384,384]{1,2,0:T(8,128)(2,1)S(1)} copy(bf16[8,384,384]{2,0,1:T(8,128)(2,1)} %all-gather.2.cloned.1.call-done) | data formatting | bytes 4718592 | tf_op jit(solution)/shard_map/while | solution.py:46
  68.9 72.0 %while.10 = (s32[]{:T(128)}, f32[4,2,384,8,32]{2,4,3,1,0:T(8,128)}, bf16[4,2,384,8,32]{2,4,3,1,0:T(8,128)(2,1)}, bf16[4,2,384,8,32]{2,4,3,1,0:T(8,128)(2,1)}, bf...) while((s32[]{:T(128)}, f32[4,2,384,8,32]{2,4,3,1,0:T(8,128)}, ...), condition=%wide.region_7.8_spmd, body=%wide.region_4.7_spmd.sunk | while | flops 319684992 | bytes 32697432 | solution.py:46
  68.9 2.4 convert_element_type.223
  71.4 10.0 %fusion.121 = (f32[2,8,384]{2,1,0:T(8,128)S(1)}, f32[2,8,384,384]{2,3,1,0:T(8,128)}) fusion(f32[2,384]{1,0:T(2,128)S(1)} %dynamic-slice_bitcast_fusion.2, f32[8,384,384]{1,2,0:T(8,128)} %convert_element_type.223, bf16[4,2,384,8,32]{2,4,3,1,0:T(8,128)(2,1)} %get-tuple-element.169, s32[]{:T(128)} %get-tuple-element.157, ...), kind=kOutput, calls=%fused_computation.109.clone.1 | convolution fusion | flops 162791808 | bytes 14970880 | tf_op jit(solution)/shard_map/while/body/eval_jaxpr/sub | solution.py:43
  81.4 5.5 %fusion.122 = f32[4,2,384,8,32]{2,4,3,1,0:T(8,128)} fusion(f32[4,2,384,8,32]{2,4,3,1,0:T(8,128)} %get-tuple-element.158, s32[]{:T(128)} %get-tuple-element.157, f32[2,8,384,384]{2,3,1,0:T(8,128)} %get-tuple-element.147, f32[2,8,384]{2,1,0:T(8,128)S(1)} %get-tuple-element.148, bf16[4,2,384,8,32]{2,4,3,1,0:T(8,128)(2,1)} %get-tuple-element.167), kind=kOutput, calls=%fused_computation.10.clone.1 | convolution fusion | flops 155713536 | bytes 10642432 | tf_op jit(solution)/shard_map/while/body/eval_jaxpr/shij,sjhd->sihd/dot_general | solution.py:44
  86.9 2.4 convert_element_type.223
  89.3 10.0 %fusion.121 = (f32[2,8,384]{2,1,0:T(8,128)S(1)}, f32[2,8,384,384]{2,3,1,0:T(8,128)}) fusion(f32[2,384]{1,0:T(2,128)S(1)} %dynamic-slice_bitcast_fusion.2, f32[8,384,384]{1,2,0:T(8,128)} %convert_element_type.223, bf16[4,2,384,8,32]{2,4,3,1,0:T(8,128)(2,1)} %get-tuple-element.169, s32[]{:T(128)} %get-tuple-element.157, ...), kind=kOutput, calls=%fused_computation.109.clone.1 | convolution fusion | flops 162791808 | bytes 14970880 | tf_op jit(solution)/shard_map/while/body/eval_jaxpr/sub | solution.py:43
  99.3 5.5 %fusion.122 = f32[4,2,384,8,32]{2,4,3,1,0:T(8,128)} fusion(f32[4,2,384,8,32]{2,4,3,1,0:T(8,128)} %get-tuple-element.158, s32[]{:T(128)} %get-tuple-element.157, f32[2,8,384,384]{2,3,1,0:T(8,128)} %get-tuple-element.147, f32[2,8,384]{2,1,0:T(8,128)S(1)} %get-tuple-element.148, bf16[4,2,384,8,32]{2,4,3,1,0:T(8,128)(2,1)} %get-tuple-element.167), kind=kOutput, calls=%fused_computation.10.clone.1 | convolution fusion | flops 155713536 | bytes 10642432 | tf_op jit(solution)/shard_map/while/body/eval_jaxpr/shij,sjhd->sihd/dot_general | solution.py:44
  104.9 2.4 convert_element_type.223
  107.3 10.0 %fusion.121 = (f32[2,8,384]{2,1,0:T(8,128)S(1)}, f32[2,8,384,384]{2,3,1,0:T(8,128)}) fusion(f32[2,384]{1,0:T(2,128)S(1)} %dynamic-slice_bitcast_fusion.2, f32[8,384,384]{1,2,0:T(8,128)} %convert_element_type.223, bf16[4,2,384,8,32]{2,4,3,1,0:T(8,128)(2,1)} %get-tuple-element.169, s32[]{:T(128)} %get-tuple-element.157, ...), kind=kOutput, calls=%fused_computation.109.clone.1 | convolution fusion | flops 162791808 | bytes 14970880 | tf_op jit(solution)/shard_map/while/body/eval_jaxpr/sub | solution.py:43
  117.3 5.5 %fusion.122 = f32[4,2,384,8,32]{2,4,3,1,0:T(8,128)} fusion(f32[4,2,384,8,32]{2,4,3,1,0:T(8,128)} %get-tuple-element.158, s32[]{:T(128)} %get-tuple-element.157, f32[2,8,384,384]{2,3,1,0:T(8,128)} %get-tuple-element.147, f32[2,8,384]{2,1,0:T(8,128)S(1)} %get-tuple-element.148, bf16[4,2,384,8,32]{2,4,3,1,0:T(8,128)(2,1)} %get-tuple-element.167), kind=kOutput, calls=%fused_computation.10.clone.1 | convolution fusion | flops 155713536 | bytes 10642432 | tf_op jit(solution)/shard_map/while/body/eval_jaxpr/shij,sjhd->sihd/dot_general | solution.py:44
  122.9 2.4 convert_element_type.223
  125.3 10.0 %fusion.121 = (f32[2,8,384]{2,1,0:T(8,128)S(1)}, f32[2,8,384,384]{2,3,1,0:T(8,128)}) fusion(f32[2,384]{1,0:T(2,128)S(1)} %dynamic-slice_bitcast_fusion.2, f32[8,384,384]{1,2,0:T(8,128)} %convert_element_type.223, bf16[4,2,384,8,32]{2,4,3,1,0:T(8,128)(2,1)} %get-tuple-element.169, s32[]{:T(128)} %get-tuple-element.157, ...), kind=kOutput, calls=%fused_computation.109.clone.1 | convolution fusion | flops 162791808 | bytes 14970880 | tf_op jit(solution)/shard_map/while/body/eval_jaxpr/sub | solution.py:43
  135.3 5.5 %fusion.122 = f32[4,2,384,8,32]{2,4,3,1,0:T(8,128)} fusion(f32[4,2,384,8,32]{2,4,3,1,0:T(8,128)} %get-tuple-element.158, s32[]{:T(128)} %get-tuple-element.157, f32[2,8,384,384]{2,3,1,0:T(8,128)} %get-tuple-element.147, f32[2,8,384]{2,1,0:T(8,128)S(1)} %get-tuple-element.148, bf16[4,2,384,8,32]{2,4,3,1,0:T(8,128)(2,1)} %get-tuple-element.167), kind=kOutput, calls=%fused_computation.10.clone.1 | convolution fusion | flops 155713536 | bytes 10642432 | tf_op jit(solution)/shard_map/while/body/eval_jaxpr/shij,sjhd->sihd/dot_general | solution.py:44
  140.9 3.3 %fusion.64 = bf16[8,384,8,32]{1,3,2,0:T(8,128)(2,1)S(1)} fusion(f32[4,2,384,8,32]{2,4,3,1,0:T(8,128)} %get-tuple-element.42, bf16[4,8,384,8,32]{2,4,3,0,1:T(8,128)(2,1)} %copy-done.4), kind=kLoop, calls=%fused_computation.67 | loop fusion | flops 4718592 | bytes 6291456 | tf_op jit(solution)/shard_map/convert_element_type | solution.py:48
  144.2 0.0 copy-start.9
  144.2 0.8 convert_reduce_fusion.2
  145.0 0.4 fusion.57
  145.5 1.1 convolution_convert_fusion
  146.7 1.7 copy-done.5
  148.4 0.2 slice.41
  148.6 0.3 multiply_reduce_fusion
  148.9 1.6 copy.76
  150.5 0.0 all-reduce.3.cloned.1.call-update
  150.5 0.0 all-reduce.5.cloned.1.call-start
  150.6 1.1 fusion.105
  151.7 1.3 copy.56
  153.0 0.5 copy.59
  153.5 34.5 %all-reduce.3.cloned.1.call-done = f32[384,8,32]{2,1,0:T(8,128)} async-done(((f32[384,8,32]{2,1,0:T(8,128)}), f32[384,8,32]{2,1,0:T(8,128)}) %all-reduce.3.cloned.1.call-update) | async-done | bytes 393232 | tf_op jit(solution)/shard_map/psum | solution.py:65
  188.0 3.8 %fusion.106 = (f32[384,8]{1,0:T(8,128)S(1)}, f32[8,384,8]{2,0,1:T(8,128)}) fusion(f32[8,384]{0,1:T(8,128)S(1)} %copy.57, bf16[8,384,32]{2,0,1:T(8,128)(2,1)} %copy.56, f32[384,8,32]{2,1,0:T(8,128)} %all-reduce.3.cloned.1.call-done, f32[384]{0:T(512)S(1)} %broadcast_add_fusion), kind=kOutput, calls=%fused_computation.112 | convolution fusion | flops 1840128 | bytes 714240 | tf_op jit(solution)/shard_map/nhd,snd->snh/dot_general | solution.py:67
  191.8 12.4 %pmax.7 = f32[384,8]{1,0:T(8,128)S(1)} all-reduce(f32[384,8]{1,0:T(8,128)S(1)} %get-tuple-element.98), channel_id=1, replica_groups=mesh['batch'=2,'seq'=4] {'seq'}, use_global_device_ids=true, to_apply=%region_14.15 | all-reduce | flops 3072 | bytes 24576 | tf_op jit(solution)/shard_map/pmax | solution.py:73
  204.1 2.1 fusion.79
  206.3 2.0 convolution_multiply_fusion
  208.4 0.0 all-reduce.5.cloned.1.call-update
  208.4 3.9 %add_divide_fusion = f32[8,384,256]{1,2,0:T(8,128)} fusion(bf16[8,384,576]{1,2,0:T(8,128)(2,1)} %copy-done.5), kind=kLoop, calls=%fused_computation.70 | loop fusion | flops 3145728 | bytes 4718592 | tf_op jit(solution)/shard_map/div | solution.py:48
  212.3 17.5 %psum.31 = f32[384,8]{1,0:T(8,128)S(1)} all-reduce(f32[384,8]{1,0:T(8,128)S(1)} %get-tuple-element.85), channel_id=1, replica_groups=mesh['batch'=2,'seq'=4] {'seq'}, use_global_device_ids=true, to_apply=%region_17.18 | all-reduce | flops 3072 | bytes 24576 | tf_op jit(solution)/shard_map/psum | solution.py:75
  229.8 20.4 %all-reduce.5.cloned.1.call-done = f32[384,8,32]{2,1,0:T(8,128)} async-done(((f32[384,8,32]{2,1,0:T(8,128)}), f32[384,8,32]{2,1,0:T(8,128)}) %all-reduce.5.cloned.1.call-update) | async-done | bytes 393232 | tf_op jit(solution)/shard_map/psum | solution.py:75
  250.2 3.0 %broadcast_divide_fusion = f32[384,8,32]{2,1,0:T(8,128)} fusion(f32[384,8,32]{2,1,0:T(8,128)} %all-reduce.5.cloned.1.call-done, f32[384,8]{1,0:T(8,128)S(1)} %psum.31), kind=kLoop, calls=%fused_computation.87 | loop fusion | flops 98304 | bytes 798720 | tf_op jit(solution)/shard_map/div | solution.py:76
  253.2 1.8 copy.60
  255.1 2.7 convert_reduce_fusion.1
  257.8 1.1 copy-done.7
  259.0 0.4 fusion.55
  259.4 6.5 %fusion.63 = bf16[8,384,256]{1,2,0:T(8,128)(2,1)} fusion(bf16[8,384,256]{1,2,0:T(8,128)(2,1)} %copy-done.7, f32[8,384]{1,0:T(8,128)S(1)} %add_rsqrt_fusion.1, f32[8,384]{1,0:T(8,128)S(1)} %broadcast_multiply_fusion.1, bf16[1024,256]{1,0:T(8,128)(2,1)S(1)} %copy-done, bf16[256,1024]{1,0:T(8,128)(2,1)S(1)} %copy-done.13), kind=kOutput, calls=%fused_computation.65 | convolution fusion | flops 3233021952 | bytes 4218880 | tf_op jit(solution)/shard_map/snf,fc->snc/dot_general | solution.py:85
  266.0 2.3 copy.63
  268.3 22.5 %all_to_all.18 = bf16[8,384,256]{2,0,1:T(8,128)(2,1)S(1)} all-to-all(bf16[8,384,256]{2,0,1:T(8,128)(2,1)S(1)} %copy.63), channel_id=1, replica_groups=mesh['batch'=2,'seq'=4] {'seq'}, dimensions={1} | all-to-all | bytes 3145728 | tf_op jit(solution)/shard_map/all_to_all | solution.py:98
  290.8 1.5 copy.65
  (42 shorter events, 0.2 us)
Async XLA Ops:
  6.5 252.9 %copy-start = (bf16[1024,256]{1,0:T(8,128)(2,1)S(1)}, bf16[1024,256]{1,0:T(8,128)(2,1)}, u32[]{:S(2)}) copy-start(bf16[1024,256]{1,0:T(8,128)(2,1)} %param.21) | copy-start | bytes 1572868
  6.5 59.1 %all-gather.2.cloned.1.call-start = ((), (), s32[]{:S(2)}) async-start(), calls=%async_computation.1 | async-start | bytes 2949120 | tf_op jit(solution)/shard_map/all_gather | solution.py:93
  12.8 12.3 %copy-start.3 = (bf16[96,384,128]{2,1,0:T(8,128)(2,1)S(1)}, bf16[96,384,128]{2,1,0:T(8,128)(2,1)}, u32[]{:S(2)}) copy-start(bf16[96,384,128]{2,1,0:T(8,128)(2,1)} %param.14) | copy-start | bytes 28311556
  12.9 12.3 %copy-start.14 = (bf16[128,8]{0,1:T(8,128)(2,1)S(1)}, bf16[128,8]{0,1:T(8,128)(2,1)}, u32[]{:S(2)}) copy-start(bf16[128,8]{0,1:T(8,128)(2,1)} %param.15) | copy-start | bytes 6148
  25.2 16.6 %copy-start.12 = (s32[8,384]{1,0:T(8,128)S(1)}, s32[8,384]{1,0:T(8,128)}, u32[]{:S(2)}) copy-start(s32[8,384]{1,0:T(8,128)} %param.13) | copy-start | bytes 36868
  41.7 2.1 copy-start.8
  41.7 146.3 %all-reduce.3.cloned.1.call-start = ((), (), s32[]{:S(2)}) async-start(), calls=%async_computation.2 | async-start | bytes 3145728 | tf_op jit(solution)/shard_map/psum | solution.py:65
  43.9 11.8 %copy-start.1 = (bf16[8,384,256]{1,2,0:T(8,128)(2,1)}, bf16[8,384,256]{1,2,0:T(8,128)(2,1)S(1)}, u32[]{:S(2)}) copy-start(bf16[8,384,256]{1,2,0:T(8,128)(2,1)S(1)} %copy.51) | copy-start | bytes 4718596
  55.7 2.7 copy-start.4
  140.9 3.3 %copy-start.2 = (bf16[8,384,256]{1,2,0:T(8,128)(2,1)S(1)}, bf16[8,384,256]{1,2,0:T(8,128)(2,1)}, u32[]{:S(2)}) copy-start(bf16[8,384,256]{1,2,0:T(8,128)(2,1)} %copy-done.1) | copy-start | bytes 4718596
  140.9 3.3 %copy-start.10 = (bf16[256,256]{1,0:T(8,128)(2,1)S(1)}, bf16[256,256]{1,0:T(8,128)(2,1)}, u32[]{:S(2)}) copy-start(bf16[256,256]{1,0:T(8,128)(2,1)} %param.17) | copy-start | bytes 393220
  144.2 1.3 copy-start.9
  146.7 1.8 copy-start.5
  150.5 99.6 %all-reduce.5.cloned.1.call-start = ((), (), s32[]{:S(2)}) async-start(), calls=%async_computation.3 | async-start | bytes 3145728 | tf_op jit(solution)/shard_map/psum | solution.py:75
  204.1 2.2 copy-start.6
  212.3 42.8 %copy-start.11 = (bf16[256,256]{1,0:T(8,128)(2,1)S(1)}, bf16[256,256]{1,0:T(8,128)(2,1)}, u32[]{:S(2)}) copy-start(bf16[256,256]{1,0:T(8,128)(2,1)} %param.19) | copy-start | bytes 393220
  255.1 4.4 %copy-start.13 = (bf16[256,1024]{1,0:T(8,128)(2,1)S(1)}, bf16[256,1024]{1,0:T(8,128)(2,1)}, u32[]{:S(2)}) copy-start(bf16[256,1024]{1,0:T(8,128)(2,1)} %param.20) | copy-start | bytes 1572868
  257.8 1.1 copy-start.7
Sparse Core Ops, SparseCore 0:
  41.8 23.7 all-gather.1
  150.7 37.2 all-reduce.2
  208.5 41.6 all-reduce.4
where the time goes:
time: 299 us
  matrix products  97.5 us (33%)
  blocking collectives  61.4 us (21%)
  waiting for transfers between devices  59.8 us (20%)
  other arithmetic  42.6 us (14%)
  local copies, waits for them, and re-layouts  23.8 us (8%)
  between operations  13.5 us (5%)
    sub x4, matrix products, tile_body(): attn_probs = jax.nn.softmax(logits, axis=-1).astype(jnp.bfloat16)  40 us
    psum x1, waiting for transfers between devices, column_attention(): q_sum, mask_count = lax.psum((q_sum, mask_count), 'seq')  34.5 us
    all_to_all x1, blocking collectives, local_block(): return lax.all_to_all(after_trans, 'seq', 1, 0, tiled=True)  22.5 us
    dot_general x4, matrix products, tile_body(): jnp.einsum('shij,sjhd->sihd', attn_probs, v_tile, preferred_element_type=...  22.2 us
    psum x1, waiting for transfers between devices, column_attention(): lax.psum((loc_den * rescale, loc_num * rescale[:, :, None]), 'seq')  20.4 us
    psum x1, blocking collectives, column_attention(): lax.psum((loc_den * rescale, loc_num * rescale[:, :, None]), 'seq')  17.5 us
    dot_general x1, matrix products, local_block(): jnp.einsum('ijc,ch->hij', layer_norm(pair_act), w_pair_bias, preferred_el...  16.5 us
    reduce_sum x4, other arithmetic, layer_norm(): var_val = jnp.mean(centered * centered, axis=-1, keepdims=True)  13.5 us
  transfers between devices with their start and end apart: 3, of which 3 were waited for; matrix products, arithmetic and copies ran while one was open for 5% of the time, Pallas kernels for 0%

commit v1 on v0

v1 whole, which is shorter than its diff:
```python
import functools

import jax
import jax.numpy as jnp
from jax import lax
from jax.experimental import pallas as pl
from jax.experimental.pallas import tpu as pltpu
from jax.sharding import PartitionSpec as P

LN_EPS = 1.0e-5
MASK_BIG = 1.0e9
MEAN_EPS = 1.0e-10
LOG2E = 1.4426950408889634

N_DEV = 4
N_LOC = 8
N_SEQ = 32
N_RES = 384
BLK = 96
N_CH = 256
N_PAIR = 128
N_HEADS = 8
HEAD_DIM = 32
SCALE = HEAD_DIM ** -0.5
Z_ROWS = 8
Z_CHUNKS = BLK // Z_ROWS
COL_BLK = 16
F32 = jnp.float32
BF16 = jnp.bfloat16
MESH = pl.DeviceIdType.MESH


def dot(a, b):
    return jnp.dot(a, b, preferred_element_type=F32)


def dot_nt(a, b):
    return lax.dot_general(a, b, (((1,), (1,)), ((), ())), preferred_element_type=F32)


def sigmoid(x):
    return 0.5 * jnp.tanh(0.5 * x) + 0.5


def layer_norm(x):
    x = x.astype(F32)
    centered = x - jnp.mean(x, axis=-1, keepdims=True)
    var = jnp.mean(centered * centered, axis=-1, keepdims=True)
    return (centered * lax.rsqrt(var + LN_EPS)).astype(BF16)


def row_kernel(e_ref, mask_ref, z_ref, w_pair_ref, w_in_ref, w_out_ref, e1_ref, mask_all_ref,
               z_buf, proj, bias_all, bias_tmp, bias_f32, q_heads, probs, gated, e1_send,
               z_sem, b_send, b_recv, r_send, r_recv, o_send, o_recv, m_send, m_recv, m_loc):
    me = lax.axis_index("seq")
    x, c = me // 2, me % 2
    peer = x * 2 + (1 - c)
    cross = (1 - x) * 2 + c
    diag = (1 - x) * 2 + (1 - c)

    barrier = pltpu.get_barrier_semaphore()
    for other in (peer, cross, diag):
        pl.semaphore_signal(barrier, inc=1, device_id={"seq": other}, device_id_type=MESH)

    def z_copy(i):
        return pltpu.make_async_copy(z_ref.at[pl.ds(i * Z_ROWS * N_RES, Z_ROWS * N_RES)], z_buf.at[i], z_sem.at[i])

    for i in range(Z_CHUNKS):
        z_copy(i).start()
    pl.semaphore_wait(barrier, 3)

    def mask_copy(k, other):
        return pltpu.make_async_remote_copy(
            src_ref=mask_ref, dst_ref=mask_all_ref.at[pl.ds(pl.multiple_of(me * N_LOC, N_LOC), N_LOC)],
            send_sem=m_send.at[k], recv_sem=m_recv.at[k], device_id={"seq": other}, device_id_type=MESH)

    mask_copies = [mask_copy(k, other) for k, other in enumerate((peer, cross, diag))]
    for copy in mask_copies:
        copy.start()
    mask_own = pltpu.make_async_copy(mask_ref, mask_all_ref.at[pl.ds(pl.multiple_of(me * N_LOC, N_LOC), N_LOC)], m_loc)
    mask_own.start()

    eye = (lax.broadcasted_iota(jnp.int32, (N_HEADS, N_HEADS), 0) == lax.broadcasted_iota(jnp.int32, (N_HEADS, N_HEADS), 1)).astype(BF16)
    w_pair_t = dot_nt(eye, w_pair_ref[...]).astype(BF16)
    rows = Z_ROWS * N_HEADS

    def bias_copy(k, other, i):
        part = bias_all.at[me, pl.ds(pl.multiple_of(i * rows, rows), rows)]
        return pltpu.make_async_remote_copy(
            src_ref=part, dst_ref=part, send_sem=b_send.at[k, i], recv_sem=b_recv.at[k, i],
            device_id={"seq": other}, device_id_type=MESH)

    def bias_chunk(i, carry):
        z_copy(i).wait()
        z_t = z_buf[i].T.astype(F32)
        centered = z_t - jnp.mean(z_t, axis=0, keepdims=True)
        var = jnp.mean(centered * centered, axis=0, keepdims=True)
        normed = (centered * lax.rsqrt(var + LN_EPS)).astype(BF16)
        out = dot(w_pair_t, normed)
        parts = [out[:, r * N_RES:(r + 1) * N_RES] for r in range(Z_ROWS)]
        bias_all[me, pl.ds(pl.multiple_of(i * rows, rows), rows)] = jnp.concatenate(parts, axis=0).astype(BF16)
        bias_copy(0, cross, i).start()
        bias_copy(1, peer, i).start()
        return carry

    lax.fori_loop(0, Z_CHUNKS, bias_chunk, 0)

    def project(s, carry):
        proj[s] = dot(layer_norm(e_ref[s]), w_in_ref[...]).astype(BF16)
        return carry

    lax.fori_loop(0, N_LOC, project, 0)

    def relay_copy(owner):
        return pltpu.make_async_remote_copy(
            src_ref=bias_all.at[owner], dst_ref=bias_all.at[owner], send_sem=r_send, recv_sem=r_recv,
            device_id={"seq": peer}, device_id_type=MESH)

    def out_copy(k, owner):
        return pltpu.make_async_remote_copy(
            src_ref=e1_send.at[k], dst_ref=e1_ref.at[pl.ds(pl.multiple_of(me * N_LOC, N_LOC), N_LOC)],
            send_sem=o_send.at[k], recv_sem=o_recv.at[k], device_id={"seq": owner}, device_id_type=MESH)

    def out_own():
        return pltpu.make_async_copy(e1_send.at[0], e1_ref.at[pl.ds(pl.multiple_of(me * N_LOC, N_LOC), N_LOC)], o_send.at[0])

    lane_head = lax.broadcasted_iota(jnp.int32, (1, N_CH), 1) // HEAD_DIM

    def block(k, carry):
        dx, dc = ((k + 1) // 2) % 2, k // 2
        owner = ((x + dx) % 2) * 2 + (c + dc) % 2

        @pl.when(k == 1)
        def _():
            def wait_chunk(i, inner):
                bias_copy(0, cross, i).wait_recv()
                return inner
            lax.fori_loop(0, Z_CHUNKS, wait_chunk, 0)
            relay_copy(cross).start()

        @pl.when(k == 2)
        def _():
            relay_copy(diag).wait_recv()

        @pl.when(k == 3)
        def _():
            def wait_chunk(i, inner):
                bias_copy(1, peer, i).wait_recv()
                return inner
            lax.fori_loop(0, Z_CHUNKS, wait_chunk, 0)

        for t in range(N_RES // 128):
            bias_tmp[t] = bias_all[owner, :, t * 128:(t + 1) * 128].astype(F32) * LOG2E
        for t in range(N_RES // 128):
            for h in range(N_HEADS):
                bias_f32[pl.ds(h * BLK, BLK), t * 128:(t + 1) * 128] = bias_tmp[t, pl.ds(h, BLK, stride=N_HEADS), :]

        start = pl.multiple_of(owner * BLK, BLK)

        def one_seq(s, inner):
            q = proj[s, pl.ds(start, BLK), 0:N_CH]
            for h in range(N_HEADS):
                q_heads[pl.ds(h * BLK, BLK)] = jnp.where(lane_head == h, q, jnp.zeros_like(q))
            logits = dot_nt(q_heads[...], proj[s, :, N_CH:2 * N_CH])
            mask_bias = (MASK_BIG * LOG2E) * (mask_ref[pl.ds(s, 1)].astype(F32) - 1.0)
            logits = logits * (SCALE * LOG2E) + bias_f32[...] + mask_bias
            top = jnp.max(logits, axis=-1, keepdims=True)
            weights = jnp.exp2(logits - top)
            total = jnp.sum(weights, axis=-1, keepdims=True)
            probs[...] = (weights * (1.0 / total)).astype(BF16)
            full = dot(probs[...], proj[s, :, 2 * N_CH:3 * N_CH])
            att = full[0:BLK]
            for h in range(1, N_HEADS):
                att = jnp.where(lane_head == h, full[h * BLK:(h + 1) * BLK], att)
            gate = sigmoid(proj[s, pl.ds(start, BLK), 3 * N_CH:4 * N_CH].astype(F32))
            gated[pl.ds(pl.multiple_of(s * BLK, BLK), BLK)] = (gate * att).astype(BF16)
            return inner

        lax.fori_loop(0, N_LOC, one_seq, 0)
        update = dot(gated[...], w_out_ref[...])
        act = e_ref[:, pl.ds(start, BLK), :].astype(F32).reshape(N_LOC * BLK, N_CH)
        e1_send[k] = (act + update).astype(BF16).reshape(N_LOC, BLK, N_CH)

        @pl.when(k == 0)
        def _():
            out_own().start()

        @pl.when(k > 0)
        def _():
            out_copy(k, owner).start()

        return carry

    lax.fori_loop(0, N_DEV, block, 0)

    out_own().wait()
    for k, owner in ((1, cross), (2, diag), (3, peer)):
        out_copy(k, owner).wait()
    for copy in mask_copies:
        copy.wait()
    mask_own.wait()
    relay_copy(cross).wait_send()

    def wait_sent(i, carry):
        bias_copy(0, cross, i).wait_send()
        bias_copy(1, peer, i).wait_send()
        return carry

    lax.fori_loop(0, Z_CHUNKS, wait_sent, 0)


def row_stage(msa_act, msa_mask, pair_act, w_pair_bias, w_row_in, w_row_out):
    vmem = pl.BlockSpec(memory_space=pltpu.VMEM)
    hbm = pl.BlockSpec(memory_space=pl.ANY)
    dma = pltpu.SemaphoreType.DMA
    return pl.pallas_call(
        row_kernel,
        out_shape=(jax.ShapeDtypeStruct((N_SEQ, BLK, N_CH), BF16), jax.ShapeDtypeStruct((N_SEQ, N_RES), jnp.int32)),
        in_specs=[vmem, vmem, hbm, vmem, vmem, vmem],
        out_specs=(hbm, hbm),
        scratch_shapes=[
            pltpu.VMEM((Z_CHUNKS, Z_ROWS * N_RES, N_PAIR), BF16),
            pltpu.VMEM((N_LOC, N_RES, 4 * N_CH), BF16),
            pltpu.VMEM((N_DEV, BLK * N_HEADS, N_RES), BF16),
            pltpu.VMEM((N_RES // 128, BLK * N_HEADS, 128), F32),
            pltpu.VMEM((BLK * N_HEADS, N_RES), F32),
            pltpu.VMEM((BLK * N_HEADS, N_CH), BF16),
            pltpu.VMEM((BLK * N_HEADS, N_RES), BF16),
            pltpu.VMEM((N_LOC * BLK, N_CH), BF16),
            pltpu.VMEM((N_DEV, N_LOC, BLK, N_CH), BF16),
            dma((Z_CHUNKS,)),
            dma((2, Z_CHUNKS)), dma((2, Z_CHUNKS)),
            dma, dma,
            dma((N_DEV,)), dma((N_DEV,)),
            dma((3,)), dma((3,)), dma,
        ],
        compiler_params=pltpu.CompilerParams(collective_id=0, has_side_effects=True, vmem_limit_bytes=60 * 2 ** 20),
        name="row_stage",
    )(msa_act, msa_mask, pair_act, w_pair_bias, w_row_in, w_row_out)


def col_kernel(e1_ref, mask_ref, w_in_ref, w_out_ref, w_t1_ref, w_t2_ref, out_ref, w_big):
    step = pl.program_id(0)
    me = lax.axis_index("seq")
    n_rows = N_SEQ * COL_BLK

    @pl.when(step == 0)
    def _():
        n_in = w_in_ref.shape[1]
        r = lax.broadcasted_iota(jnp.int32, (n_in, 4 * N_CH), 0)
        col = lax.broadcasted_iota(jnp.int32, (n_in, 4 * N_CH), 1)
        part = col // N_CH
        src = jnp.where(part == 0, col, jnp.where(part == 3, col - 3 * N_CH + N_CH + 2 * HEAD_DIM,
                                                  N_CH + (part - 1) * HEAD_DIM + col % HEAD_DIM))
        w_big[...] = dot(w_in_ref[...], (r == src).astype(BF16)).astype(BF16)

    x = e1_ref[...].reshape(n_rows, N_CH)
    proj = dot(layer_norm(x), w_big[...]).astype(BF16)
    first = me * BLK + step * COL_BLK
    lane = lax.broadcasted_iota(jnp.int32, (N_SEQ, COL_BLK, N_RES), 2)
    res = lax.broadcasted_iota(jnp.int32, (N_SEQ, COL_BLK, N_RES), 1)
    picked = jnp.where(lane == first + res, mask_ref[...].astype(F32)[:, None, :], 0.0).astype(BF16).reshape(n_rows, N_RES)
    mask = dot(picked, jnp.ones((N_RES, N_CH), BF16)).reshape(N_SEQ, COL_BLK, N_CH)

    q = proj[:, 0:N_CH].astype(F32).reshape(N_SEQ, COL_BLK, N_CH)
    k = proj[:, N_CH:2 * N_CH].astype(F32).reshape(N_SEQ, COL_BLK, N_CH)
    v = proj[:, 2 * N_CH:3 * N_CH].astype(F32).reshape(N_SEQ, COL_BLK, N_CH)
    g = proj[:, 3 * N_CH:4 * N_CH].astype(F32).reshape(N_SEQ, COL_BLK, N_CH)
    q_mean = (jnp.sum(mask * q, axis=0) / (jnp.sum(mask, axis=0) + MEAN_EPS)).astype(BF16).astype(F32)
    prod = (q_mean[None] * k).reshape(n_rows, N_CH)
    high = prod.astype(BF16)
    low = (prod - high.astype(F32)).astype(BF16)
    same_head = (lax.broadcasted_iota(jnp.int32, (N_CH, N_CH), 0) // HEAD_DIM == lax.broadcasted_iota(jnp.int32, (N_CH, N_CH), 1) // HEAD_DIM).astype(BF16)
    logits = (dot(high, same_head) + dot(low, same_head)).reshape(N_SEQ, COL_BLK, N_CH)
    logits = logits * (SCALE * LOG2E) + (MASK_BIG * LOG2E) * (mask - 1.0)
    weights = jnp.exp2(logits - jnp.max(logits, axis=0)[None])
    o = jnp.sum(weights * v, axis=0) / jnp.sum(weights, axis=0)
    gated = (sigmoid(g) * o[None]).astype(BF16).reshape(n_rows, N_CH)
    e2 = (x.astype(F32) + dot(gated, w_out_ref[...])).astype(BF16)
    hidden = jnp.maximum(dot(layer_norm(e2), w_t1_ref[...]), 0.0).astype(BF16)
    e3 = (e2.astype(F32) + dot(hidden, w_t2_ref[...])).astype(BF16)
    out_ref[...] = e3.reshape(N_SEQ, COL_BLK, N_CH)


def col_stage(e1, mask_all, w_col_in, w_col_out, w_trans_in, w_trans_out):
    whole = lambda a: pl.BlockSpec(a.shape, lambda i: (0, 0))
    blk = pl.BlockSpec((N_SEQ, COL_BLK, N_CH), lambda i: (0, i, 0))
    return pl.pallas_call(
        col_kernel,
        grid=(BLK // COL_BLK,),
        out_shape=jax.ShapeDtypeStruct((N_SEQ, BLK, N_CH), BF16),
        in_specs=[blk, whole(mask_all), whole(w_col_in), whole(w_col_out), whole(w_trans_in), whole(w_trans_out)],
        out_specs=blk,
        scratch_shapes=[pltpu.VMEM((N_CH, 4 * N_CH), BF16)],
        compiler_params=pltpu.CompilerParams(dimension_semantics=("arbitrary",), vmem_limit_bytes=60 * 2 ** 20),
        name="col_stage",
    )(e1, mask_all, w_col_in, w_col_out, w_trans_in, w_trans_out)


def solution(mesh):
    def local_block(msa_act, msa_mask, pair_act, w_pair_bias, w_row_in, w_row_out, w_col_in, w_col_out, w_trans_in, w_trans_out):
        pairs = pair_act.reshape(BLK * N_RES, N_PAIR)
        e1, mask_all = row_stage(msa_act, msa_mask, pairs, w_pair_bias, w_row_in, w_row_out)
        return col_stage(e1, mask_all, w_col_in, w_col_out, w_trans_in, w_trans_out)

    rows_spec = P(('batch', 'seq'))
    return jax.shard_map(local_block, mesh=mesh, in_specs=(rows_spec, rows_spec, rows_spec, P(), P(), P(), P(), P(), P(), P()), out_specs=P('batch', 'seq'), check_vma=False)
```

time: 299 us -> 81.9 us (0.27)
  matrix products: 97.5 us -> 0 us
  Pallas kernels: 0 us -> 78.5 us
  blocking collectives: 61.4 us -> 0 us
  waiting for transfers between devices: 59.8 us -> 0 us
  other arithmetic: 42.6 us -> 0 us
  local copies, waits for them, and re-layouts: 23.8 us -> 3.25 us
  between operations: 13.5 us -> 0.01 us
    pallas_call x0 -> x2, Pallas kernels: none -> 78.5 us  [the longest x1 57.4 us: row_stage(): pl.pallas_call(row_kernel, out_shape=(jax.ShapeDtypeStruct((N_SEQ, BLK, N...]
    dot_general x12 -> x0, matrix products: 57.5 us -> none  [the longest x4 22.2 us: tile_body(): jnp.einsum('shij,sjhd->sihd', attn_probs, v_tile, preferred_element_type=...]
    psum x2 -> x0, waiting for transfers between devices: 54.9 us -> none  [the longest x1 34.5 us: column_attention(): q_sum, mask_count = lax.psum((q_sum, mask_count), 'seq')]
    sub x4 -> x0, matrix products: 40 us -> none  [tile_body(): attn_probs = jax.nn.softmax(logits, axis=-1).astype(jnp.bfloat16)]
    psum x2 -> x0, blocking collectives: 26.5 us -> none  [the longest x1 17.5 us: column_attention(): lax.psum((loc_den * rescale, loc_num * rescale[:, :, None]), 'seq')]
    all_to_all x1 -> x0, blocking collectives: 22.5 us -> none  [local_block(): return lax.all_to_all(after_trans, 'seq', 1, 0, tiled=True)]
    reduce_sum x8 -> x0, other arithmetic: 22.2 us -> none  [the longest x4 13.5 us: layer_norm(): var_val = jnp.mean(centered * centered, axis=-1, keepdims=True)]
    convert_element_type x5 -> x0, other arithmetic: 13 us -> none  [the longest x4 9.71 us: tile_body(): logits = logits + bias_hij[None] + m_tile[:, None, None, :]]
  transfers between devices with their start and end apart: 3 -> 0, of which waited for: 3 -> 0; matrix products, arithmetic and copies ran while one was open for 5% -> 0% of each run, Pallas kernels for 0% -> 0%
where the time goes in v1:
time: 81.9 us; the launch traced here: 81.7 us
  Pallas kernels  78.5 us (96%)
  local copies, waits for them, and re-layouts  3.25 us (4%)
    pallas_call x1, Pallas kernels, row_stage(): pl.pallas_call(row_kernel, out_shape=(jax.ShapeDtypeStruct((N_SEQ, BLK, N...  57.4 us
    pallas_call x1, Pallas kernels, col_stage(): pl.pallas_call(col_kernel, grid=(BLK // COL_BLK,), out_shape=jax.ShapeDty...  21.1 us
    unnamed x2, local copies, waits for them, and re-layouts  3.25 us

profile of v1, /device:TPU:0, one launch (start us, length us, event | category | flops | bytes accessed | tf_op | source)
XLA Modules:
  0.0 81.7 jit_solution(13165996013243812676)
XLA Ops:
  0.0 1.4 %copy.11.w_pair_ref = bf16[128,8]{1,0:T(8,128)(2,1)} copy(bf16[128,8]{0,1:T(8,128)(2,1)} %param.13) | data formatting | bytes 4096 | tf_op args[3]
  1.4 1.9 %copy.12.w_in_ref = bf16[256,576]{1,0:T(8,128)(2,1)} copy(bf16[256,576]{0,1:T(8,128)(2,1)} %param.16) | data formatting | bytes 589824 | tf_op args[6]
  3.3 57.4 %row_stage.1 = (bf16[32,96,256]{2,1,0:T(8,128)(2,1)}, s32[32,384]{1,0:T(8,128)}) custom-call(bf16[8,384,256]{2,1,0:T(8,128)(2,1)} %e_ref.1, s32[8,384]{1,0:T(8,128)} %mask_ref.1, bf16[36864,128]{1,0:T(8,128)(2,1)} %bitcast.1, bf16[128,8]{1,0:T(8,128)(2,1)} %copy.11.w_pair_ref, bf16[256,1024]{1,0:T(8,128)(2,1)} %w_in_ref.2, bf16[256,256]{1,0:T(8,128)(2,1)} %w_out_ref.2), custom_call_target="tpu_custom_call" | custom-call | tf_op jit(solution)/shard_map/row_stage/pallas_call | solution.py:216
  60.6 21.1 %col_stage.1 = bf16[32,96,256]{2,1,0:T(8,128)(2,1)} custom-call(bf16[32,96,256]{2,1,0:T(8,128)(2,1)} %get-tuple-element.7.e1_ref, s32[32,384]{1,0:T(8,128)} %get-tuple-element.8.mask_ref, bf16[256,576]{1,0:T(8,128)(2,1)} %copy.12.w_in_ref, bf16[256,256]{1,0:T(8,128)(2,1)} %w_out_ref.3, bf16[256,1024]{1,0:T(8,128)(2,1)} %w_t1_ref.1, bf16[1024,256]{1,0:T(8,128)(2,1)} %w_t2_ref.1), custom_call_target="tpu_custom_call" | custom-call | tf_op jit(solution)/shard_map/col_stage/pallas_call | solution.py:288
